TPU v7x, 256 devices: a whole 4x4x8 slice. The times are simulated.
256 devices in a mesh: site: 64 (over z, x, core), dom: 4 (over y).
Axes of the slice: x: 4, y: 4, z: 8, core: 2. Of those that a mesh axis runs over, the one named last changes fastest.
Arguments:
- top_partial: float32 [16, 61, 4, 65536], P(None, None, 'dom', 'site'), may hold values from 0.001 to 1
- bottom_partial: float32 [16, 61, 4, 65536], P(None, None, 'dom', 'site'), may hold values from 0.001 to 1
- left_vectors: float32 [256, 61, 61], P('dom'), may hold values from 0.05 to 1
- right_vectors: float32 [256, 61, 61], P('dom'), may hold values from 0.05 to 1
- decay_rates: float32 [256, 61], P('dom'), may hold values from 0.05 to 8
- state_weights: float32 [256, 61], P('dom'), may hold values from 0.002 to 0.05
- part_rates: float32 [256], P('dom'), may hold values from 0.3 to 3
- branch_lengths: float32 [1997], replicated, may hold values from 0.02 to 0.5
- pattern_weights: int32 [4, 65536], P('dom', 'site'), may hold values from 0 to 9
- block_partition: int32 [4, 512], P('dom', 'site'), may hold values from 0 to 255
- chosen_branches: int32 [16], replicated, may hold values from 0 to 1996, as said below
Outputs:
- site_loglik: float32 [16, 4, 65536], P(None, 'dom', 'site')
- part_derivs: float32 [2, 16, 256], P(None, None, 'dom')
- new_lengths: float32 [1997], replicated
Inputs may be any that keep to these rules, and one draw needn't show every extreme that they name: `chosen_branches`: distinct branch numbers.
All inputs are finite; a program needn't handle non-finite values.
Results may differ from a plain program's by a relative error of at most 0.0003.
Values sent between devices are 32-bit elements; how exact they have to be, the bound alone decides.
A program may use at most 64 MiB of HBM per device.

v0:
```python
import math
import jax
import jax.numpy as jnp
from jax import lax
from jax.sharding import PartitionSpec as P

BLK = 128


def in_one_piece(arrays, axis, split_dim, concat_dim, along):
    widths = [math.prod(a.shape[along:]) for a in arrays]
    both = jnp.concatenate(
        [a.reshape(*a.shape[:along], w) for a, w in zip(arrays, widths)], axis=along
    )
    out = lax.all_to_all(both, axis, split_axis=split_dim, concat_axis=concat_dim, tiled=True)
    parts = jnp.split(out, [sum(widths[:k]) for k in range(1, len(widths))], axis=along)
    return tuple((b.reshape(*out.shape[:along], *a.shape[along:]) for a, b in zip(arrays, parts)))


def cut_along(x, dim, count):
    dims = x.shape
    parts = x.reshape(*dims[:dim], count, dims[dim] // count, *dims[dim + 1 :])
    return jnp.moveaxis(parts, dim, 0)


def sum_at_owner(x, axis, dim):
    count = lax.axis_size(axis)
    parts = lax.all_to_all(cut_along(x, dim, count), axis, 0, 0, tiled=True)
    return jnp.sum(parts, axis=0)


def copy_for_each(x, axis):
    count = lax.axis_size(axis)
    return lax.all_to_all(jnp.broadcast_to(x[None], (count, *x.shape)), axis, 0, 0, tiled=True)


def of_everyone(x, axis):
    return copy_for_each(x, axis).sum(axis=0)


def project(upper, lower, vec_left, vec_right, state_w):
    scaled = upper * jnp.transpose(state_w)[None, :, :, None]
    lefts = jnp.einsum("binl,nik->bknl", scaled, vec_left, precision=lax.Precision.HIGHEST)
    rights = jnp.einsum("nkj,bjnl->bknl", vec_right, lower, precision=lax.Precision.HIGHEST)
    return (lefts, rights)


def finish(lefts, rights, exponent, times, weight_f):
    joint = lefts * rights
    expo = jnp.transpose(exponent)[None, :, :, None]
    decayed = joint * jnp.exp(expo * times[:, None, None, None])
    like_zero = jnp.sum(decayed, axis=1)
    like_one = jnp.sum(decayed * expo, axis=1)
    like_two = jnp.sum(decayed * expo * expo, axis=1)
    first = like_one / like_zero
    second = like_two / like_zero - first * first
    loglik = weight_f[None] * jnp.log(like_zero)
    sums = jnp.stack(
        [jnp.sum(weight_f[None] * first, axis=-1), jnp.sum(weight_f[None] * second, axis=-1)]
    )
    return (loglik, sums)


def on_device(
    top_partial,
    bottom_partial,
    left_vectors,
    right_vectors,
    decay_rates,
    state_weights,
    part_rates,
    branch_lengths,
    pattern_weights,
    block_partition,
    chosen_branches,
):
    times = branch_lengths[chosen_branches]
    branches = top_partial.shape[0]
    states = top_partial.shape[1]
    sites_here = top_partial.shape[3]
    nblocks = sites_here // BLK
    upper = top_partial.reshape(branches, states, nblocks, BLK)
    lower = bottom_partial.reshape(branches, states, nblocks, BLK)
    blocks = block_partition[0]
    owned = left_vectors.shape[0]
    groups = lax.axis_size("dom")
    parts_all = owned * groups
    wanted = lax.all_gather(block_partition, "dom", axis=0, tiled=True)
    relative = wanted - lax.axis_index("dom") * owned
    inside = jnp.logical_and(relative >= 0, relative < owned).astype(jnp.float32)
    clipped = jnp.clip(relative, 0, owned - 1)
    send_left = left_vectors[clipped] * inside[:, :, None, None]
    send_right = right_vectors[clipped] * inside[:, :, None, None]
    send_decay = decay_rates[clipped] * inside[:, :, None]
    send_weight = state_weights[clipped] * inside[:, :, None]
    send_rate = part_rates[clipped] * inside
    received = in_one_piece(
        (send_left, send_right, send_decay, send_weight, send_rate), "dom", 0, 0, 2
    )
    vec_left = jnp.sum(received[0], axis=0)
    vec_right = jnp.sum(received[1], axis=0)
    decay_b = jnp.sum(received[2], axis=0)
    weight_b = jnp.sum(received[3], axis=0)
    rate_b = jnp.sum(received[4], axis=0)
    exponent = -decay_b * rate_b[:, None]
    lefts, rights = project(upper, lower, vec_left, vec_right, weight_b)
    weight_f = pattern_weights[0].astype(jnp.float32).reshape(nblocks, BLK)
    loglik, sums = finish(lefts, rights, exponent, times, weight_f)
    onehot = (blocks[:, None] == jnp.arange(parts_all, dtype=jnp.int32)[None, :]).astype(
        jnp.float32
    )
    part_local = jnp.einsum("abn,np->abp", sums, onehot, precision=lax.Precision.HIGHEST)
    share = sum_at_owner(part_local, "dom", 2)
    share = of_everyone(share, "site")
    totals = of_everyone(jnp.sum(share, axis=2), "dom")
    updated = times - totals[0] / totals[1]
    new_lengths = branch_lengths.at[chosen_branches].set(updated)
    return (loglik.reshape(branches, 1, sites_here), share, new_lengths)


def solution(mesh):
    return jax.shard_map(
        on_device,
        mesh=mesh,
        in_specs=(
            P(None, None, "dom", "site"),
            P(None, None, "dom", "site"),
            P("dom", None, None),
            P("dom", None, None),
            P("dom", None),
            P("dom", None),
            P("dom"),
            P(),
            P("dom", "site"),
            P("dom", "site"),
            P(),
        ),
        out_specs=(P(None, "dom", "site"), P(None, None, "dom"), P()),
        check_vma=False,
    )
```

profile of v0, /device:TPU:2, one launch (start us, length us, event | category | flops | bytes accessed | tf_op | source)
XLA Modules:
  0.0 121.1 jit_solution(9104302624612339698)
XLA Ops:
  1.5 10.1 %all-gather = s32[4,1,8]{2,1,0:T(1,128)S(1)} all-gather(s32[1,1,8]{2,1,0:T(1,128)} %bitcast.49), channel_id=1, replica_groups=mesh['site'=64,'dom'=4] {'dom'}, dimensions={0}, use_global_device_ids=true | all-gather | bytes 160 | tf_op jit(solution)/shard_map/all_gather | solution.py:88
  11.7 1.4 %gather_fusion.4 = f32[32]{0:T(128)S(1)} fusion(f32[64]{0:T(128)} %param.17, s32[1024]{0:T(1024)S(1)} %pad_clamp_fusion.1), kind=kCustom, calls=%fused_computation.4 | custom fusion | bytes 384 | tf_op jit(solution)/shard_map/gather | solution.py:96
  13.8 2.7 %gather_fusion = f32[32,61,61]{2,0,1:T(8,128)S(1)} fusion(f32[64,61,61]{2,0,1:T(8,128)S(1)} %copy-done, s32[1024]{0:T(1024)S(1)} %pad_clamp_fusion.1), kind=kCustom, calls=%fused_computation | custom fusion | bytes 952704 | tf_op jit(solution)/shard_map/gather | solution.py:92
  16.5 1.6 %copy.60 = f32[32,61,61]{2,1,0:T(8,128)} copy(f32[32,61,61]{2,0,1:T(8,128)S(1)} %gather_fusion) | data formatting | bytes 952576 | tf_op jit(solution)/shard_map/gather | solution.py:92
  18.1 1.7 %gather.23 = f32[4,8,3721]{2,1,0:T(8,128)S(1)} reshape(f32[32,61,61]{2,1,0:T(8,128)} %copy.60) | data formatting | bytes 952576 | tf_op jit(solution)/shard_map/gather | solution.py:92
  19.8 4.0 %gather_fusion.1 = f32[32,61,61]{2,0,1:T(8,128)S(1)} fusion(f32[64,61,61]{2,0,1:T(8,128)} %param.14, s32[1024]{0:T(1024)S(1)} %pad_clamp_fusion.1), kind=kCustom, calls=%fused_computation.1 | custom fusion | bytes 952704 | tf_op jit(solution)/shard_map/gather | solution.py:93
  23.9 1.6 %copy.61 = f32[32,61,61]{2,1,0:T(8,128)} copy(f32[32,61,61]{2,0,1:T(8,128)S(1)} %gather_fusion.1) | data formatting | bytes 952576 | tf_op jit(solution)/shard_map/gather | solution.py:93
  25.4 1.7 %gather.25 = f32[4,8,3721]{2,1,0:T(8,128)S(1)} reshape(f32[32,61,61]{2,1,0:T(8,128)} %copy.61) | data formatting | bytes 952576 | tf_op jit(solution)/shard_map/gather | solution.py:93
  27.8 1.3 %gather_fusion.3 = f32[32,61]{1,0:T(8,128)S(1)} fusion(f32[64,61]{1,0:T(8,128)} %param.16, s32[1024]{0:T(1024)S(1)} %pad_clamp_fusion.1), kind=kCustom, calls=%fused_computation.3 | custom fusion | bytes 15744 | tf_op jit(solution)/shard_map/gather | solution.py:95
  29.9 0.9 broadcast_multiply_fusion
  30.9 2.2 %concatenate.3 = f32[4,8,7565]{2,1,0:T(8,128)} concatenate(f32[4,8,3721]{2,1,0:T(8,128)} %get-tuple-element.29, f32[4,8,3721]{2,1,0:T(8,128)S(1)} %get-tuple-element.28, f32[4,8,61]{2,1,0:T(8,128)S(1)} %get-tuple-element.27, f32[4,8,61]{2,1,0:T(8,128)S(1)} %get-tuple-element.26, f32[4,8,1]{2,1,0:T(8,128)S(1)} %copy.62), dimensions={2} | concatenate | bytes 1936640 | tf_op jit(solution)/shard_map/concatenate | solution.py:12
  33.1 3.5 %all-to-all-start = ((f32[4,8,7565]{2,1,0:T(8,128)}), f32[4,8,7565]{2,1,0:T(8,128)S(1)}, u32[]{:S(2)}, u32[]{:S(2)}) async-start(f32[4,8,7565]{2,1,0:T(8,128)} %concatenate.3), calls=%async_computation | async-start | bytes 1966080 | tf_op jit(solution)/shard_map/all_to_all | solution.py:15
  38.6 11.0 %all-to-all-done = f32[4,8,7565]{2,1,0:T(8,128)S(1)} async-done(((f32[4,8,7565]{2,1,0:T(8,128)}), f32[4,8,7565]{2,1,0:T(8,128)S(1)}, u32[]{:S(2)}, u32[]{:S(2)}) %all-to-all-start) | async-done | bytes 968352 | tf_op jit(solution)/shard_map/all_to_all | solution.py:15
  50.1 1.0 reduce_sum.131
  51.5 6.8 %fusion = f32[8,61,16,128]{3,1,2,0:T(8,128)S(1)} fusion(f32[16,61,8,128]{3,2,1,0:T(8,128)} %bitcast.41, f32[8,61,61,1]{2,1,0,3:T(8,128)S(1)} %reshape.171), kind=kOutput, calls=%fused_computation.8 | convolution fusion | flops 731578368 | bytes 8114464 | tf_op jit(solution)/shard_map/nkj,bjnl->bknl/dot_general | solution.py:44
  58.3 6.4 %multiply_reduce_fusion.1 = (f32[16,8,128]{2,0,1:T(8,128)S(1)}, f32[16,8,128]{2,0,1:T(8,128)S(1)}, f32[16,8,128]{2,0,1:T(8,128)S(1)}) fusion(f32[61,8]{0,1:T(8,128)S(1)} %multiply_bitcast_fusion, f32[16,61,8]{1,0,2:T(8,128)S(1)} %multiply_exponential_fusion, f32[8,61,16,128]{3,1,2,0:T(8,128)S(1)} %fusion, f32[16,61,8,128]{3,2,1,0:T(8,128)S(1)} %bitcast.51, ...), kind=kOutput, calls=%fused_computation.13 | convolution fusion | flops 739524608 | bytes 8346208 | tf_op jit(solution)/shard_map/binl,nik->bknl/dot_general | solution.py:43
  65.3 7.8 %all_to_all.20 = f32[4,1,2048]{2,1,0:T(1,128)S(1)} all-to-all(f32[4,1,2048]{2,1,0:T(1,128)S(1)} %reshape.174), channel_id=1, replica_groups=mesh['site'=64,'dom'=4] {'dom'}, dimensions={0} | all-to-all | bytes 65536 | tf_op jit(solution)/shard_map/all_to_all | solution.py:28
  74.6 1.4 %reshape.176 = f32[64,1,2048]{2,1,0:T(1,128)} reshape(f32[64,2,16,64]{3,2,1,0:T(8,128)S(1)} %broadcast_in_dim.10) | data formatting | bytes 1048576
  76.0 12.1 %all-to-all-start.2 = ((f32[64,1,2048]{2,1,0:T(1,128)}), f32[64,1,2048]{2,1,0:T(1,128)S(1)}, u32[]{:S(2)}, u32[]{:S(2)}) async-start(f32[64,1,2048]{2,1,0:T(1,128)} %reshape.176), calls=%async_computation.2 | async-start | bytes 1048576 | tf_op jit(solution)/shard_map/all_to_all | solution.py:34
  88.2 17.5 %all-to-all-done.2 = f32[64,1,2048]{2,1,0:T(1,128)S(1)} async-done(((f32[64,1,2048]{2,1,0:T(1,128)}), f32[64,1,2048]{2,1,0:T(1,128)S(1)}, u32[]{:S(2)}, u32[]{:S(2)}) %all-to-all-start.2) | async-done | bytes 524320 | tf_op jit(solution)/shard_map/all_to_all | solution.py:34
  105.7 2.8 %reduce.5 = f32[64,2048]{1,0:T(8,128)} reduce(f32[64,1,2048]{2,1,0:T(1,128)S(1)} %all-to-all-done.2, f32[]{:T(128)} %broadcast.90), dimensions={1}, to_apply=%all_to_all.14.reduce_sub_computation | reduce | bytes 1048580 | tf_op jit(solution)/shard_map/all_to_all | solution.py:34
  108.5 1.5 %reshape.177 = f32[64,2,16,64]{3,2,1,0:T(8,128)S(1)} reshape(f32[64,2048]{1,0:T(8,128)} %reduce.5) | data formatting | bytes 1048576
  111.3 3.2 %all-to-all-start.3 = ((f32[4,2,16]{2,1,0:T(2,128)}), f32[4,2,16]{2,1,0:T(2,128)S(1)}, u32[]{:S(2)}, u32[]{:S(2)}) async-start(f32[4,2,16]{2,1,0:T(2,128)} %broadcast_in_dim.11), calls=%async_computation.3 | async-start | bytes 8192 | tf_op jit(solution)/shard_map/all_to_all | solution.py:34
  115.2 4.5 %all-to-all-done.3 = f32[4,2,16]{2,1,0:T(2,128)S(1)} async-done(((f32[4,2,16]{2,1,0:T(2,128)}), f32[4,2,16]{2,1,0:T(2,128)S(1)}, u32[]{:S(2)}, u32[]{:S(2)}) %all-to-all-start.3) | async-done | bytes 544 | tf_op jit(solution)/shard_map/all_to_all | solution.py:34
  (53 shorter events, 11.3 us)
Async XLA Ops:
  0.6 13.2 %copy-start = (f32[64,61,61]{2,0,1:T(8,128)S(1)}, f32[64,61,61]{2,0,1:T(8,128)}, u32[]{:S(2)}) copy-start(f32[64,61,61]{2,0,1:T(8,128)} %param.13) | copy-start | bytes 2857732
  19.8 7.4 %copy-start.2 = (f32[64,61]{1,0:T(8,128)S(1)}, f32[64,61]{1,0:T(8,128)}, u32[]{:S(2)}) copy-start(f32[64,61]{1,0:T(8,128)} %param.15) | copy-start | bytes 46852
  33.1 16.5 %all-to-all-start = ((f32[4,8,7565]{2,1,0:T(8,128)}), f32[4,8,7565]{2,1,0:T(8,128)S(1)}, u32[]{:S(2)}, u32[]{:S(2)}) async-start(f32[4,8,7565]{2,1,0:T(8,128)} %concatenate.3), calls=%async_computation | async-start | bytes 1966080 | tf_op jit(solution)/shard_map/all_to_all | solution.py:15
  51.5 6.8 %copy-start.3 = (f32[8,61,61]{2,1,0:T(8,128)S(1)}, f32[8,61,61]{2,1,0:T(8,128)}, u32[]{:S(2)}) copy-start(f32[8,61,61]{2,1,0:T(8,128)} %reduce_sum.131) | copy-start | bytes 357220
  51.5 6.8 %copy-start.5 = (f32[16,61,1,1024]{3,2,1,0:T(1,128)S(1)}, f32[16,61,1,1024]{3,2,1,0:T(1,128)}, u32[]{:S(2)}) copy-start(f32[16,61,1,1024]{3,2,1,0:T(1,128)} %param.11) | copy-start | bytes 11993092
  58.3 6.5 %copy-start.4 = (s32[1,8]{1,0:T(1,128)S(1)}, s32[1,8]{1,0:T(1,128)}, u32[]{:S(2)}) copy-start(s32[1,8]{1,0:T(1,128)} %param.20) | copy-start | bytes 100
  76.0 29.7 %all-to-all-start.2 = ((f32[64,1,2048]{2,1,0:T(1,128)}), f32[64,1,2048]{2,1,0:T(1,128)S(1)}, u32[]{:S(2)}, u32[]{:S(2)}) async-start(f32[64,1,2048]{2,1,0:T(1,128)} %reshape.176), calls=%async_computation.2 | async-start | bytes 1048576 | tf_op jit(solution)/shard_map/all_to_all | solution.py:34
  111.3 8.5 %all-to-all-start.3 = ((f32[4,2,16]{2,1,0:T(2,128)}), f32[4,2,16]{2,1,0:T(2,128)S(1)}, u32[]{:S(2)}, u32[]{:S(2)}) async-start(f32[4,2,16]{2,1,0:T(2,128)} %broadcast_in_dim.11), calls=%async_computation.3 | async-start | bytes 8192 | tf_op jit(solution)/shard_map/all_to_all | solution.py:34
  120.5 0.6 copy-start.1
where the time goes:
time: 122 us; the launch traced here: 121 us
  waiting for transfers between devices  33 us (27%)
  local copies, waits for them, and re-layouts  29 us (24%)
  starting transfers between devices  18.9 us (15%)
  blocking collectives  17.9 us (15%)
  matrix products  13.4 us (11%)
  other arithmetic  8 us (7%)
    all_to_all x2, waiting for transfers between devices, copy_for_each(): lax.all_to_all(jnp.broadcast_to(x[None], (count, *x.shape)), axis, 0, 0,...  22 us
    all_to_all x2, starting transfers between devices, copy_for_each(): lax.all_to_all(jnp.broadcast_to(x[None], (count, *x.shape)), axis, 0, 0,...  15.4 us
    all_to_all x1, waiting for transfers between devices, in_one_piece(): lax.all_to_all(both, axis, split_axis=split_dim, concat_axis=concat_dim,...  11 us
    all_gather x1, blocking collectives, on_device(): wanted = lax.all_gather(block_partition, 'dom', axis=0, tiled=True)  10.1 us
    all_to_all x1, blocking collectives, sum_at_owner(): parts = lax.all_to_all(cut_along(x, dim, count), axis, 0, 0, tiled=True)  7.8 us
    gather x3, local copies, waits for them, and re-layouts, on_device(): send_right = right_vectors[clipped] * inside[:, :, None, None]  7.34 us
    dot_general x1, matrix products, project(): jnp.einsum('nkj,bjnl->bknl', vec_right, lower, precision=lax.Precision.HI...  6.79 us
    dot_general x1, matrix products, project(): jnp.einsum('binl,nik->bknl', scaled, vec_left, precision=lax.Precision.HI...  6.36 us
  transfers between devices with their start and end apart: 3, of which 3 were waited for; matrix products, arithmetic and copies ran while one was open for 2% of the time, Pallas kernels for 0%

commit v1 on v0

--- a/solution.py
+++ b/solution.py
@@ -5,6 +5,28 @@
 from jax.sharding import PartitionSpec as P
 
 BLK = 128
+
+
+def in_order(pieces, dim):
+    dims = list(pieces.shape[1:])
+    dims[dim] *= pieces.shape[0]
+    return jnp.moveaxis(pieces, 0, dim).reshape(dims)
+
+
+def ring_gather(value, axis, dim):
+    devices = lax.axis_size(axis)
+    pairs = [(i, (i + 1) % devices) for i in range(devices)]
+    back = [(b, a) for a, b in pairs]
+    lower, upper = ([], [])
+    for step in range(devices - 1):
+        if step % 2 == 0:
+            lower.append(lax.ppermute(lower[-1] if lower else value, axis, pairs))
+        else:
+            upper.append(lax.ppermute(upper[-1] if upper else value, axis, back))
+    pieces = jnp.stack([*lower[::-1], value, *upper])
+    shift = lax.axis_index(axis) - len(lower)
+    pieces = pieces[(jnp.arange(devices) - shift) % devices]
+    return in_order(pieces, dim)
 
 
 def in_one_piece(arrays, axis, split_dim, concat_dim, along):
@@ -85,7 +107,7 @@
     owned = left_vectors.shape[0]
     groups = lax.axis_size("dom")
     parts_all = owned * groups
-    wanted = lax.all_gather(block_partition, "dom", axis=0, tiled=True)
+    wanted = ring_gather(block_partition, "dom", 0)
     relative = wanted - lax.axis_index("dom") * owned
     inside = jnp.logical_and(relative >= 0, relative < owned).astype(jnp.float32)
     clipped = jnp.clip(relative, 0, owned - 1)

time: 122 us -> 124 us (1.016)
  blocking collectives: 17.9 us -> 7.8 us
  waiting for transfers between devices: 33 us -> 42.7 us
  starting transfers between devices: 18.9 us -> 21.8 us
    all_gather x1 -> x0, blocking collectives: 10.1 us -> none  [on_device(): wanted = lax.all_gather(block_partition, 'dom', axis=0, tiled=True)]
    ppermute x0 -> x3, waiting for transfers between devices: none -> 9.66 us  [the longest x2 9.66 us: ring_gather(): lower.append(lax.ppermute(lower[-1] if lower else value, axis, pairs))]
    ppermute x0 -> x3, starting transfers between devices: none -> 3.02 us  [the longest x1 3.01 us: ring_gather(): upper.append(lax.ppermute(upper[-1] if upper else value, axis, back))]
    gather x3, local copies, waits for them, and re-layouts: 6.02 us -> 8.23 us  [on_device(): send_left = left_vectors[clipped] * inside[:, :, None, None]]
    gather x3, local copies, waits for them, and re-layouts: 7.34 us -> 6.03 us  [on_device(): send_right = right_vectors[clipped] * inside[:, :, None, None]]
    unnamed x18 -> x22, local copies, waits for them, and re-layouts: 5.26 us -> 5.27 us
  transfers between devices with their start and end apart: 3 -> 6, of which waited for: 3 -> 5; matrix products, arithmetic and copies ran while one was open for 2% -> 2% of each run, Pallas kernels for 0% -> 0%
where the time goes in v1:
time: 124 us; the launch traced here: 123 us
  waiting for transfers between devices  42.7 us (34%)
  local copies, waits for them, and re-layouts  29.1 us (23%)
  starting transfers between devices  21.8 us (18%)
  matrix products  13.4 us (11%)
  blocking collectives  7.8 us (6%)
  other arithmetic  7.41 us (6%)
    all_to_all x2, waiting for transfers between devices, copy_for_each(): lax.all_to_all(jnp.broadcast_to(x[None], (count, *x.shape)), axis, 0, 0,...  22 us
    all_to_all x2, starting transfers between devices, copy_for_each(): lax.all_to_all(jnp.broadcast_to(x[None], (count, *x.shape)), axis, 0, 0,...  15.1 us
    all_to_all x1, waiting for transfers between devices, in_one_piece(): lax.all_to_all(both, axis, split_axis=split_dim, concat_axis=concat_dim,...  11 us
    ppermute x2, waiting for transfers between devices, ring_gather(): lower.append(lax.ppermute(lower[-1] if lower else value, axis, pairs))  9.66 us
    gather x3, local copies, waits for them, and re-layouts, on_device(): send_left = left_vectors[clipped] * inside[:, :, None, None]  8.23 us
    all_to_all x1, blocking collectives, sum_at_owner(): parts = lax.all_to_all(cut_along(x, dim, count), axis, 0, 0, tiled=True)  7.8 us
    dot_general x1, matrix products, project(): jnp.einsum('nkj,bjnl->bknl', vec_right, lower, precision=lax.Precision.HI...  6.8 us
    dot_general x1, matrix products, project(): jnp.einsum('binl,nik->bknl', scaled, vec_left, precision=lax.Precision.HI...  6.37 us
  transfers between devices with their start and end apart: 6, of which 5 were waited for; matrix products, arithmetic and copies ran while one was open for 2% of the time, Pallas kernels for 0%

profile of v1, /device:TPU:2, one launch (start us, length us, event | category | flops | bytes accessed | tf_op | source)
XLA Modules:
  0.0 123.2 jit_solution(8612370782264748251)
XLA Ops:
  1.5 3.0 %collective-permute-start.2 = (s32[1,8]{1,0:T(1,128)}, s32[1,8]{1,0:T(1,128)S(1)}, u32[]{:S(2)}, u32[]{:S(2)}) collective-permute-start(s32[1,8]{1,0:T(1,128)} %param.20), channel_id=1, source_target_pairs={{1,0},{2,1},{3,2},{0,3},{5,4},{6,5},{7,6},{4,7},{9,8},{10,9},{11,1... | collective-permute-start | bytes 104 | tf_op jit(solution)/shard_map/ppermute | solution.py:25
  4.5 4.9 %collective-permute-done = s32[1,8]{1,0:T(1,128)S(1)} collective-permute-done((s32[1,8]{1,0:T(1,128)}, s32[1,8]{1,0:T(1,128)S(1)}, u32[]{:S(2)}, u32[]{:S(2)}) %collective-permute-start) | collective-permute-done | bytes 64 | tf_op jit(solution)/shard_map/ppermute | solution.py:23
  9.4 4.8 %collective-permute-done.1 = s32[1,8]{1,0:T(1,128)S(1)} collective-permute-done((s32[1,8]{1,0:T(1,128)S(1)}, s32[1,8]{1,0:T(1,128)S(1)}, u32[]{:S(2)}, u32[]{:S(2)}) %collective-permute-start.1) | collective-permute-done | bytes 64 | tf_op jit(solution)/shard_map/ppermute | solution.py:23
  15.5 2.7 %gather_fusion.2 = f32[32,61,61]{2,0,1:T(8,128)S(1)} fusion(f32[64,61,61]{2,0,1:T(8,128)S(1)} %copy-done, s32[1024]{0:T(1024)S(1)} %pad_clamp_fusion.1), kind=kCustom, calls=%fused_computation.2 | custom fusion | bytes 952704 | tf_op jit(solution)/shard_map/gather | solution.py:115
  18.3 1.6 %copy.65 = f32[32,61,61]{2,1,0:T(8,128)} copy(f32[32,61,61]{2,0,1:T(8,128)S(1)} %gather_fusion.2) | data formatting | bytes 952576 | tf_op jit(solution)/shard_map/gather | solution.py:115
  19.9 1.7 %gather.31 = f32[4,8,3721]{2,1,0:T(8,128)S(1)} reshape(f32[32,61,61]{2,1,0:T(8,128)} %copy.65) | data formatting | bytes 952576 | tf_op jit(solution)/shard_map/gather | solution.py:115
  21.6 4.9 %gather_fusion.1 = f32[32,61,61]{2,0,1:T(8,128)S(1)} fusion(f32[64,61,61]{2,0,1:T(8,128)} %param.13, s32[1024]{0:T(1024)S(1)} %pad_clamp_fusion.1), kind=kCustom, calls=%fused_computation.1 | custom fusion | bytes 952704 | tf_op jit(solution)/shard_map/gather | solution.py:114
  26.5 1.6 %copy.64 = f32[32,61,61]{2,1,0:T(8,128)} copy(f32[32,61,61]{2,0,1:T(8,128)S(1)} %gather_fusion.1) | data formatting | bytes 952576 | tf_op jit(solution)/shard_map/gather | solution.py:114
  28.1 1.7 %gather.29 = f32[4,8,3721]{2,1,0:T(8,128)S(1)} reshape(f32[32,61,61]{2,1,0:T(8,128)} %copy.64) | data formatting | bytes 952576 | tf_op jit(solution)/shard_map/gather | solution.py:114
  30.4 1.3 %gather_fusion.3 = f32[32,61]{1,0:T(8,128)S(1)} fusion(f32[64,61]{1,0:T(8,128)} %param.15, s32[1024]{0:T(1024)S(1)} %pad_clamp_fusion.1), kind=kCustom, calls=%fused_computation.3 | custom fusion | bytes 15744 | tf_op jit(solution)/shard_map/gather | solution.py:116
  33.7 2.2 %concatenate.3 = f32[4,8,7565]{2,1,0:T(8,128)} concatenate(f32[4,8,3721]{2,1,0:T(8,128)} %get-tuple-element.29, f32[4,8,3721]{2,1,0:T(8,128)S(1)} %get-tuple-element.28, f32[4,8,61]{2,1,0:T(8,128)S(1)} %get-tuple-element.27, f32[4,8,61]{2,1,0:T(8,128)S(1)} %get-tuple-element.26, f32[4,8,1]{2,1,0:T(8,128)S(1)} %broadcast_select_fusion), dimensions={2} | concatenate | bytes 1936640 | tf_op jit(solution)/shard_map/concatenate | solution.py:34
  35.9 3.7 %all-to-all-start = ((f32[4,8,7565]{2,1,0:T(8,128)}), f32[4,8,7565]{2,1,0:T(8,128)S(1)}, u32[]{:S(2)}, u32[]{:S(2)}) async-start(f32[4,8,7565]{2,1,0:T(8,128)} %concatenate.3), calls=%async_computation | async-start | bytes 1966080 | tf_op jit(solution)/shard_map/all_to_all | solution.py:37
  41.0 11.0 %all-to-all-done = f32[4,8,7565]{2,1,0:T(8,128)S(1)} async-done(((f32[4,8,7565]{2,1,0:T(8,128)}), f32[4,8,7565]{2,1,0:T(8,128)S(1)}, u32[]{:S(2)}, u32[]{:S(2)}) %all-to-all-start) | async-done | bytes 968352 | tf_op jit(solution)/shard_map/all_to_all | solution.py:37
  52.5 1.0 reduce_sum.131
  53.9 6.8 %fusion = f32[8,61,16,128]{3,1,2,0:T(8,128)S(1)} fusion(f32[16,61,8,128]{3,2,1,0:T(8,128)} %bitcast.46, f32[8,61,61,1]{2,1,0,3:T(8,128)S(1)} %reshape.299), kind=kOutput, calls=%fused_computation.9 | convolution fusion | flops 731578368 | bytes 8114464 | tf_op jit(solution)/shard_map/nkj,bjnl->bknl/dot_general | solution.py:66
  60.8 6.4 %multiply_reduce_fusion.1 = (f32[16,8,128]{2,0,1:T(8,128)S(1)}, f32[16,8,128]{2,0,1:T(8,128)S(1)}, f32[16,8,128]{2,0,1:T(8,128)S(1)}) fusion(f32[61,8]{0,1:T(8,128)S(1)} %multiply_bitcast_fusion, f32[16,61,8]{1,0,2:T(8,128)S(1)} %multiply_exponential_fusion, f32[8,61,16,128]{3,1,2,0:T(8,128)S(1)} %fusion, f32[16,61,8,128]{3,2,1,0:T(8,128)S(1)} %bitcast.60, ...), kind=kOutput, calls=%fused_computation.14 | convolution fusion | flops 739524608 | bytes 8346208 | tf_op jit(solution)/shard_map/binl,nik->bknl/dot_general | solution.py:65
  67.7 7.8 %all_to_all.20 = f32[4,1,2048]{2,1,0:T(1,128)S(1)} all-to-all(f32[4,1,2048]{2,1,0:T(1,128)S(1)} %reshape.302), channel_id=1, replica_groups=mesh['site'=64,'dom'=4] {'dom'}, dimensions={0} | all-to-all | bytes 65536 | tf_op jit(solution)/shard_map/all_to_all | solution.py:50
  77.0 1.4 %reshape.304 = f32[64,1,2048]{2,1,0:T(1,128)} reshape(f32[64,2,16,64]{3,2,1,0:T(8,128)S(1)} %broadcast_in_dim.7) | data formatting | bytes 1048576
  78.4 11.9 %all-to-all-start.2 = ((f32[64,1,2048]{2,1,0:T(1,128)}), f32[64,1,2048]{2,1,0:T(1,128)S(1)}, u32[]{:S(2)}, u32[]{:S(2)}) async-start(f32[64,1,2048]{2,1,0:T(1,128)} %reshape.304), calls=%async_computation.2 | async-start | bytes 1048576 | tf_op jit(solution)/shard_map/all_to_all | solution.py:56
  90.4 17.5 %all-to-all-done.2 = f32[64,1,2048]{2,1,0:T(1,128)S(1)} async-done(((f32[64,1,2048]{2,1,0:T(1,128)}), f32[64,1,2048]{2,1,0:T(1,128)S(1)}, u32[]{:S(2)}, u32[]{:S(2)}) %all-to-all-start.2) | async-done | bytes 524320 | tf_op jit(solution)/shard_map/all_to_all | solution.py:56
  107.9 2.8 %reduce.5 = f32[64,2048]{1,0:T(8,128)} reduce(f32[64,1,2048]{2,1,0:T(1,128)S(1)} %all-to-all-done.2, f32[]{:T(128)} %broadcast.260), dimensions={1}, to_apply=%all_to_all.14.reduce_sub_computation | reduce | bytes 1048580 | tf_op jit(solution)/shard_map/all_to_all | solution.py:56
  110.7 1.5 %reshape.305 = f32[64,2,16,64]{3,2,1,0:T(8,128)S(1)} reshape(f32[64,2048]{1,0:T(8,128)} %reduce.5) | data formatting | bytes 1048576
  113.4 3.2 %all-to-all-start.3 = ((f32[4,2,16]{2,1,0:T(2,128)}), f32[4,2,16]{2,1,0:T(2,128)S(1)}, u32[]{:S(2)}, u32[]{:S(2)}) async-start(f32[4,2,16]{2,1,0:T(2,128)} %broadcast_in_dim.8), calls=%async_computation.3 | async-start | bytes 8192 | tf_op jit(solution)/shard_map/all_to_all | solution.py:56
  117.4 4.5 %all-to-all-done.3 = f32[4,2,16]{2,1,0:T(2,128)S(1)} async-done(((f32[4,2,16]{2,1,0:T(2,128)}), f32[4,2,16]{2,1,0:T(2,128)S(1)}, u32[]{:S(2)}, u32[]{:S(2)}) %all-to-all-start.3) | async-done | bytes 544 | tf_op jit(solution)/shard_map/all_to_all | solution.py:56
  (64 shorter events, 12.3 us)
Async XLA Ops:
  0.6 14.9 %copy-start = (f32[64,61,61]{2,0,1:T(8,128)S(1)}, f32[64,61,61]{2,0,1:T(8,128)}, u32[]{:S(2)}) copy-start(f32[64,61,61]{2,0,1:T(8,128)} %param.14) | copy-start | bytes 2857732
  1.5 7.9 %collective-permute-start.2 = (s32[1,8]{1,0:T(1,128)}, s32[1,8]{1,0:T(1,128)S(1)}, u32[]{:S(2)}, u32[]{:S(2)}) collective-permute-start(s32[1,8]{1,0:T(1,128)} %param.20), channel_id=1, source_target_pairs={{1,0},{2,1},{3,2},{0,3},{5,4},{6,5},{7,6},{4,7},{9,8},{10,9},{11,1... | collective-permute-start | bytes 104 | tf_op jit(solution)/shard_map/ppermute | solution.py:25
  4.5 4.9 %collective-permute-start = (s32[1,8]{1,0:T(1,128)}, s32[1,8]{1,0:T(1,128)S(1)}, u32[]{:S(2)}, u32[]{:S(2)}) collective-permute-start(s32[1,8]{1,0:T(1,128)} %param.20), channel_id=1, source_target_pairs={{0,1},{1,2},{2,3},{3,0},{4,5},{5,6},{6,7},{7,4},{8,9},{9,10},{10,1... | collective-permute-start | bytes 104 | tf_op jit(solution)/shard_map/ppermute | solution.py:23
  9.4 4.8 %collective-permute-start.1 = (s32[1,8]{1,0:T(1,128)S(1)}, s32[1,8]{1,0:T(1,128)S(1)}, u32[]{:S(2)}, u32[]{:S(2)}) collective-permute-start(s32[1,8]{1,0:T(1,128)S(1)} %collective-permute-done), channel_id=1, source_target_pairs={{0,1},{1,2},{2,3},{3,0},{4,5},{5,6},{6,7},{7,4},{8,9},{9,10},{10,1... | collective-permute-start | bytes 104 | tf_op jit(solution)/shard_map/ppermute | solution.py:23
  21.6 8.3 %copy-start.3 = (f32[64,61]{1,0:T(8,128)S(1)}, f32[64,61]{1,0:T(8,128)}, u32[]{:S(2)}) copy-start(f32[64,61]{1,0:T(8,128)} %param.16) | copy-start | bytes 46852
  26.5 5.4 %copy-start.1 = (f32[64]{0:T(128)S(1)}, f32[64]{0:T(128)}, u32[]{:S(2)}) copy-start(f32[64]{0:T(128)} %param.17) | copy-start | bytes 772
  30.4 9.2 %copy-start.5 = (s32[1,1024]{1,0:T(1,128)S(1)}, s32[1,1024]{1,0:T(1,128)}, u32[]{:S(2)}) copy-start(s32[1,1024]{1,0:T(1,128)} %param.19) | copy-start | bytes 12292
  35.9 16.1 %all-to-all-start = ((f32[4,8,7565]{2,1,0:T(8,128)}), f32[4,8,7565]{2,1,0:T(8,128)S(1)}, u32[]{:S(2)}, u32[]{:S(2)}) async-start(f32[4,8,7565]{2,1,0:T(8,128)} %concatenate.3), calls=%async_computation | async-start | bytes 1966080 | tf_op jit(solution)/shard_map/all_to_all | solution.py:37
  53.9 6.8 %copy-start.4 = (f32[8,61,61]{2,1,0:T(8,128)S(1)}, f32[8,61,61]{2,1,0:T(8,128)}, u32[]{:S(2)}) copy-start(f32[8,61,61]{2,1,0:T(8,128)} %reduce_sum.131) | copy-start | bytes 357220
  53.9 6.8 %copy-start.7 = (f32[16,61,1,1024]{3,2,1,0:T(1,128)S(1)}, f32[16,61,1,1024]{3,2,1,0:T(1,128)}, u32[]{:S(2)}) copy-start(f32[16,61,1,1024]{3,2,1,0:T(1,128)} %param.11) | copy-start | bytes 11993092
  60.7 6.5 %copy-start.6 = (s32[1,8]{1,0:T(1,128)S(1)}, s32[1,8]{1,0:T(1,128)}, u32[]{:S(2)}) copy-start(s32[1,8]{1,0:T(1,128)} %param.20) | copy-start | bytes 100
  78.4 29.4 %all-to-all-start.2 = ((f32[64,1,2048]{2,1,0:T(1,128)}), f32[64,1,2048]{2,1,0:T(1,128)S(1)}, u32[]{:S(2)}, u32[]{:S(2)}) async-start(f32[64,1,2048]{2,1,0:T(1,128)} %reshape.304), calls=%async_computation.2 | async-start | bytes 1048576 | tf_op jit(solution)/shard_map/all_to_all | solution.py:56
  113.4 8.5 %all-to-all-start.3 = ((f32[4,2,16]{2,1,0:T(2,128)}), f32[4,2,16]{2,1,0:T(2,128)S(1)}, u32[]{:S(2)}, u32[]{:S(2)}) async-start(f32[4,2,16]{2,1,0:T(2,128)} %broadcast_in_dim.8), calls=%async_computation.3 | async-start | bytes 8192 | tf_op jit(solution)/shard_map/all_to_all | solution.py:56
  122.6 0.6 copy-start.2
